TPU v7x, 32 devices: a whole 2x2x4 slice. The times are simulated.
32 devices in a mesh: unit: 4 (over z), lat: 2 (over y), lon: 2 (over core), lev: 2 (over x).
Axes of the slice: x: 2, y: 2, z: 4, core: 2. Of those that a mesh axis runs over, the one named last changes fastest.
Arguments:
- tracer: float32 [32, 128, 64, 128], P(('unit', 'lat'), 'lon', 'lev'), parts along dimension 0, may hold values from 0.2 to 1.8
- crowding: float32 [32, 128, 64, 128], P(('unit', 'lat'), 'lon', 'lev'), parts along dimension 0, may hold values from 0.5 to 2
Outputs:
- column_sum: float32 [32, 128, 64, 128], P(('unit', 'lat'), 'lon', 'lev'), parts along dimension 0
- tracer_end: float32 [32, 128, 64, 128], P(('unit', 'lat'), 'lon', 'lev'), parts along dimension 0
There are 4 independent parts, one for each index of `unit`. A program takes and returns all parts, laid end to end along the dimension named above; each array names one. Nothing has to cross between parts.
All inputs are finite; a program needn't handle non-finite values.
Results may differ from a plain program's by a relative error of at most 0.00002.
Values sent between devices are 32-bit elements; how exact they have to be, the bound alone decides.
A program may use at most 128 MiB of HBM per device.

v0:
```python
import jax
import jax.numpy as jnp
from jax import lax
from jax.sharding import PartitionSpec as P

STEPS = 4


def with_halo(array, sides, width):
    for axis, dim in sides:
        devices, length = (lax.axis_size(axis), array.shape[dim])
        up = [(i, (i + 1) % devices) for i in range(devices - 1)]
        down = [(j, i) for i, j in up]
        last = lax.slice_in_dim(array, length - width, length, axis=dim)
        first = lax.slice_in_dim(array, 0, width, axis=dim)
        before = lax.ppermute(last, axis, up)
        after = lax.ppermute(first, axis, down)
        array = jnp.concatenate([before, array, after], axis=dim)
    return array


def prefix(array, axis, combine, identity):
    devices, here = (lax.axis_size(axis), lax.axis_index(axis))
    everything = lax.all_gather(array, axis)
    start = jnp.broadcast_to(jnp.asarray(identity, array.dtype), array.shape)

    def turn(k, before):
        reached = k < here
        new = combine(before, everything[k])
        return jnp.where(reached, new, before)

    return lax.fori_loop(0, devices, turn, start)


def without_rim(values, dims):
    for dim in dims:
        values = lax.slice_in_dim(values, 1, values.shape[dim] - 1, axis=dim)
    return values


def shifted_cells(values, dim, start, dims):
    others = [other for other in dims if other != dim]
    values = without_rim(values, others)
    return lax.slice_in_dim(values, start, start + values.shape[dim] - 2, axis=dim)


def march_step(padded, crowding):
    middle = without_rim(padded, (0, 1, 2))
    lower = [shifted_cells(padded, dim, 0, (0, 1, 2)) for dim in (0, 1, 2)]
    upper = [shifted_cells(padded, dim, 2, (0, 1, 2)) for dim in (0, 1, 2)]
    spread = lower[0] + upper[0] + lower[1] + upper[1] + lower[2] + upper[2] - 6.0 * middle
    return middle + 0.1 * spread + 0.2 * middle * (1.0 - middle * crowding)


def on_device(tracer, crowding):
    for step in range(STEPS):
        padded = with_halo(tracer, (("lat", 0), ("lon", 1), ("lev", 2)), 1)
        tracer = march_step(padded, crowding)
    here = jnp.cumsum(tracer, axis=0)
    total = lax.slice_in_dim(here, here.shape[0] - 1, here.shape[0], axis=0)

    def add_pair(earlier_total, later_total):
        return earlier_total + later_total

    below = prefix(total, "lat", add_pair, jnp.zeros_like(total))
    column_sum = (here + below) / (tracer.shape[0] * lax.axis_size("lat"))
    return (column_sum, tracer)


def solution(mesh):
    return jax.shard_map(
        on_device,
        mesh=mesh,
        in_specs=(P(("unit", "lat"), "lon", "lev", None), P(("unit", "lat"), "lon", "lev", None)),
        out_specs=(P(("unit", "lat"), "lon", "lev", None), P(("unit", "lat"), "lon", "lev", None)),
        check_vma=False,
    )
```

profile of v0, /device:TPU:0, one launch (start us, length us, event | category | flops | bytes accessed | tf_op | source)
XLA Modules:
  0.0 272.6 jit_solution(10311514362742806973)
XLA Ops:
  7.2 1.9 fusion.40
  9.1 5.0 %collective-permute-start = (f32[1,64,32,128]{3,2,1,0:T(8,128)S(1)}, f32[1,64,32,128]{3,2,1,0:T(8,128)S(1)}, u32[]{:S(2)}, u32[]{:S(2)}) collective-permute-start(f32[1,64,32,128]{3,2,1,0:T(8,128)S(1)} %get-tuple-element.142), channel_id=1, source_target_pairs={{0,4},{1,5},{2,6},{3,7},{8,12},{9,13},{10,14},{11,15},{16,20},{17,... | collective-permute-start | bytes 3145736 | tf_op jit(solution)/shard_map/ppermute | solution.py:16
  15.4 21.0 %collective-permute-done = f32[1,64,32,128]{3,2,1,0:T(8,128)S(1)} collective-permute-done((f32[1,64,32,128]{3,2,1,0:T(8,128)S(1)}, f32[1,64,32,128]{3,2,1,0:T(8,128)S(1)}, u32[]{:S(2)}, u32[]{:S(2)}) %collective-permute-start) | collective-permute-done | bytes 1048608 | tf_op jit(solution)/shard_map/ppermute | solution.py:16
  36.9 3.6 %collective-permute-done.1 = f32[1,64,32,128]{3,2,1,0:T(8,128)S(1)} collective-permute-done((f32[1,64,32,128]{3,2,1,0:T(8,128)S(1)}, f32[1,64,32,128]{3,2,1,0:T(8,128)S(1)}, u32[]{:S(2)}, u32[]{:S(2)}) %collective-permute-start.1) | collective-permute-done | bytes 1048608 | tf_op jit(solution)/shard_map/ppermute | solution.py:17
  43.6 1.9 collective-permute-done.3
  45.8 3.4 %collective-permute-start.4 = (f32[6,66,1,128]{3,1,2,0:T(8,128)S(1)}, f32[6,66,1,128]{3,1,2,0:T(8,128)S(1)}, u32[]{:S(2)}, u32[]{:S(2)}) collective-permute-start(f32[6,66,1,128]{3,1,2,0:T(8,128)S(1)} %copy.23), channel_id=1, source_target_pairs={{0,1},{2,3},{4,5},{6,7},{8,9},{10,11},{12,13},{14,15},{16,17},{18,... | collective-permute-start | bytes 608264 | tf_op jit(solution)/shard_map/ppermute | solution.py:16
  50.5 3.6 %collective-permute-done.4 = f32[6,66,1,128]{3,1,2,0:T(8,128)S(1)} collective-permute-done((f32[6,66,1,128]{3,1,2,0:T(8,128)S(1)}, f32[6,66,1,128]{3,1,2,0:T(8,128)S(1)}, u32[]{:S(2)}, u32[]{:S(2)}) %collective-permute-start.4) | collective-permute-done | bytes 202784 | tf_op jit(solution)/shard_map/ppermute | solution.py:16
  54.4 3.9 %collective-permute-done.5 = f32[6,66,1,128]{3,1,2,0:T(8,128)S(1)} collective-permute-done((f32[6,66,1,128]{3,1,2,0:T(8,128)S(1)}, f32[6,66,1,128]{3,1,2,0:T(8,128)S(1)}, u32[]{:S(2)}, u32[]{:S(2)}) %collective-permute-start.5) | collective-permute-done | bytes 202784 | tf_op jit(solution)/shard_map/ppermute | solution.py:17
  58.5 9.3 %fusion.31 = f32[4,64,32,128]{3,2,1,0:T(8,128)S(1)} fusion(f32[4,64,32,128]{3,2,1,0:T(8,128)} %param.4, f32[6,66,1,128]{3,2,1,0:T(1,128)S(1)} %copy.26, f32[6,1,32,128]{3,2,1,0:T(8,128)} %copy-done.4, f32[6,64,32,128]{3,2,1,0:T(8,128)S(1)} %constant_dynamic-update-slice_fusion, f32[6,1,32,128]{3,2,1,0:T(8,128)S(1)} %collective-permute-done.2, ...), kind=kLoop, calls=%fused_computation.87 | loop fusion | flops 25165824 | bytes 21573632 | tf_op jit(solution)/shard_map/add | solution.py:52
  70.8 20.3 %collective-permute-done.6 = f32[1,64,32,128]{3,2,1,0:T(8,128)S(1)} collective-permute-done((f32[1,64,32,128]{3,2,1,0:T(8,128)S(1)}, f32[1,64,32,128]{3,2,1,0:T(8,128)S(1)}, u32[]{:S(2)}, u32[]{:S(2)}) %collective-permute-start.6) | collective-permute-done | bytes 1048608 | tf_op jit(solution)/shard_map/ppermute | solution.py:16
  91.1 4.2 %collective-permute-done.7 = f32[1,64,32,128]{3,2,1,0:T(8,128)S(1)} collective-permute-done((f32[1,64,32,128]{3,2,1,0:T(8,128)S(1)}, f32[1,64,32,128]{3,2,1,0:T(8,128)S(1)}, u32[]{:S(2)}, u32[]{:S(2)}) %collective-permute-start.7) | collective-permute-done | bytes 1048608 | tf_op jit(solution)/shard_map/ppermute | solution.py:17
  98.0 1.9 collective-permute-done.9
  102.9 3.8 %collective-permute-done.10 = f32[6,66,1,128]{3,1,2,0:T(8,128)S(1)} collective-permute-done((f32[6,66,1,128]{3,1,2,0:T(8,128)S(1)}, f32[6,66,1,128]{3,1,2,0:T(8,128)S(1)}, u32[]{:S(2)}, u32[]{:S(2)}) %collective-permute-start.10) | collective-permute-done | bytes 202784 | tf_op jit(solution)/shard_map/ppermute | solution.py:16
  106.9 3.9 %collective-permute-done.11 = f32[6,66,1,128]{3,1,2,0:T(8,128)S(1)} collective-permute-done((f32[6,66,1,128]{3,1,2,0:T(8,128)S(1)}, f32[6,66,1,128]{3,1,2,0:T(8,128)S(1)}, u32[]{:S(2)}, u32[]{:S(2)}) %collective-permute-start.11) | collective-permute-done | bytes 202784 | tf_op jit(solution)/shard_map/ppermute | solution.py:17
  111.1 7.2 %fusion.22 = f32[4,64,32,128]{3,2,1,0:T(8,128)S(1)} fusion(f32[4,64,32,128]{3,2,1,0:T(8,128)S(1)} %fusion.31, f32[6,66,1,128]{3,2,1,0:T(1,128)S(1)} %copy.30, f32[6,1,32,128]{3,2,1,0:T(8,128)S(1)} %collective-permute-done.9, f32[6,1,32,128]{3,2,1,0:T(8,128)S(1)} %collective-permute-done.8, f32[1,64,32,128]{3,2,1,0:T(8,128)S(1)} %collective-permute-done.7, ...), kind=kLoop, calls=%fused_computation.60 | loop fusion | flops 33554432 | bytes 15282176 | tf_op jit(solution)/shard_map/add | solution.py:52
  121.3 20.5 %collective-permute-done.12 = f32[1,64,32,128]{3,2,1,0:T(8,128)S(1)} collective-permute-done((f32[1,64,32,128]{3,2,1,0:T(8,128)S(1)}, f32[1,64,32,128]{3,2,1,0:T(8,128)S(1)}, u32[]{:S(2)}, u32[]{:S(2)}) %collective-permute-start.12) | collective-permute-done | bytes 1048608 | tf_op jit(solution)/shard_map/ppermute | solution.py:16
  141.8 4.2 %collective-permute-done.13 = f32[1,64,32,128]{3,2,1,0:T(8,128)S(1)} collective-permute-done((f32[1,64,32,128]{3,2,1,0:T(8,128)S(1)}, f32[1,64,32,128]{3,2,1,0:T(8,128)S(1)}, u32[]{:S(2)}, u32[]{:S(2)}) %collective-permute-start.13) | collective-permute-done | bytes 1048608 | tf_op jit(solution)/shard_map/ppermute | solution.py:17
  148.6 1.9 collective-permute-done.15
  153.6 3.8 %collective-permute-done.16 = f32[6,66,1,128]{3,1,2,0:T(8,128)S(1)} collective-permute-done((f32[6,66,1,128]{3,1,2,0:T(8,128)S(1)}, f32[6,66,1,128]{3,1,2,0:T(8,128)S(1)}, u32[]{:S(2)}, u32[]{:S(2)}) %collective-permute-start.16) | collective-permute-done | bytes 202784 | tf_op jit(solution)/shard_map/ppermute | solution.py:16
  157.6 3.9 %collective-permute-done.17 = f32[6,66,1,128]{3,1,2,0:T(8,128)S(1)} collective-permute-done((f32[6,66,1,128]{3,1,2,0:T(8,128)S(1)}, f32[6,66,1,128]{3,1,2,0:T(8,128)S(1)}, u32[]{:S(2)}, u32[]{:S(2)}) %collective-permute-start.17) | collective-permute-done | bytes 202784 | tf_op jit(solution)/shard_map/ppermute | solution.py:17
  161.7 7.2 %fusion.13 = f32[4,64,32,128]{3,2,1,0:T(8,128)S(1)} fusion(f32[4,64,32,128]{3,2,1,0:T(8,128)S(1)} %fusion.22, f32[6,66,1,128]{3,2,1,0:T(1,128)S(1)} %copy.34, f32[6,1,32,128]{3,2,1,0:T(8,128)S(1)} %collective-permute-done.15, f32[6,1,32,128]{3,2,1,0:T(8,128)S(1)} %collective-permute-done.14, f32[1,64,32,128]{3,2,1,0:T(8,128)S(1)} %collective-permute-done.13, ...), kind=kLoop, calls=%fused_computation.33 | loop fusion | flops 33554432 | bytes 15282176 | tf_op jit(solution)/shard_map/add | solution.py:52
  171.9 20.5 %collective-permute-done.18 = f32[1,64,32,128]{3,2,1,0:T(8,128)S(1)} collective-permute-done((f32[1,64,32,128]{3,2,1,0:T(8,128)S(1)}, f32[1,64,32,128]{3,2,1,0:T(8,128)S(1)}, u32[]{:S(2)}, u32[]{:S(2)}) %collective-permute-start.18) | collective-permute-done | bytes 1048608 | tf_op jit(solution)/shard_map/ppermute | solution.py:16
  192.4 4.2 %collective-permute-done.19 = f32[1,64,32,128]{3,2,1,0:T(8,128)S(1)} collective-permute-done((f32[1,64,32,128]{3,2,1,0:T(8,128)S(1)}, f32[1,64,32,128]{3,2,1,0:T(8,128)S(1)}, u32[]{:S(2)}, u32[]{:S(2)}) %collective-permute-start.19) | collective-permute-done | bytes 1048608 | tf_op jit(solution)/shard_map/ppermute | solution.py:17
  199.2 1.9 collective-permute-done.21
  204.4 3.6 %collective-permute-done.22 = f32[6,66,1,128]{3,1,2,0:T(8,128)S(1)} collective-permute-done((f32[6,66,1,128]{3,1,2,0:T(8,128)S(1)}, f32[6,66,1,128]{3,1,2,0:T(8,128)S(1)}, u32[]{:S(2)}, u32[]{:S(2)}) %collective-permute-start.22) | collective-permute-done | bytes 202784 | tf_op jit(solution)/shard_map/ppermute | solution.py:16
  208.2 3.9 %collective-permute-done.23 = f32[6,66,1,128]{3,1,2,0:T(8,128)S(1)} collective-permute-done((f32[6,66,1,128]{3,1,2,0:T(8,128)S(1)}, f32[6,66,1,128]{3,1,2,0:T(8,128)S(1)}, u32[]{:S(2)}, u32[]{:S(2)}) %collective-permute-start.23) | collective-permute-done | bytes 202784 | tf_op jit(solution)/shard_map/ppermute | solution.py:17
  212.3 7.2 %fusion.4 = f32[4,64,32,128]{3,2,1,0:T(8,128)S(1)} fusion(f32[4,64,32,128]{3,2,1,0:T(8,128)S(1)} %fusion.13, f32[6,66,1,128]{3,2,1,0:T(1,128)S(1)} %copy.38, f32[6,1,32,128]{3,2,1,0:T(8,128)S(1)} %collective-permute-done.21, f32[6,1,32,128]{3,2,1,0:T(8,128)S(1)} %collective-permute-done.20, f32[1,64,32,128]{3,2,1,0:T(8,128)S(1)} %collective-permute-done.19, ...), kind=kLoop, calls=%fused_computation.6 | loop fusion | flops 33554432 | bytes 15282176 | tf_op jit(solution)/shard_map/add | solution.py:52
  219.5 2.9 %fusion.41 = f32[4,64,32,128]{3,2,1,0:T(8,128)} fusion(f32[4,64,32,128]{3,2,1,0:T(8,128)S(1)} %fusion.4), kind=kOutput, calls=%fused_computation.137 | output fusion | flops 3145728 | bytes 8388608 | tf_op jit(solution)/shard_map/jit(cumsum)/reduce_window_sum | solution.py:59
  222.8 2.3 slice.360
  225.1 32.6 %all-gather.3.cloned.1.call-done = f32[2,64,32,128]{3,2,1,0:T(8,128)} async-done(((f32[1,64,32,128]{3,2,1,0:T(8,128)}), f32[2,64,32,128]{3,2,1,0:T(8,128)}) %all-gather.3.cloned.1.call-update) | async-done | bytes 2097168 | tf_op jit(solution)/shard_map/all_gather | solution.py:24
  257.7 3.2 %while.14 = (s32[]{:T(128)}, f32[1,64,32,128]{3,2,1,0:T(8,128)S(1)}, s32[]{:T(128)}, f32[2,1,64,32,128]{4,3,2,1,0:T(8,128)}, s32[]{:T(128)}, /*index=5*/s32[]{:T(128)}) while((s32[]{:T(128)}, f32[1,64,32,128]{3,2,1,0:T(8,128)S(1)}, s32[]{:T(128)}, f32[2,1,64,32,128]{4,3,2,1,0:T(8,128)}, s32[]{:T(128)}, /*index=5*/s32[]{:T(128)}) %tuple.57), condition=%wide.region_2.3_spmd.clone, body=%wide.region_1.2_spmd.clone.sunk | while | flops 786436 | bytes 3145821 | solution.py:32
  260.9 4.9 %add_multiply_fusion = f32[4,64,32,128]{3,2,1,0:T(8,128)} fusion(f32[4,64,32,128]{3,2,1,0:T(8,128)} %fusion.41, f32[64,32,128]{2,1,0:T(8,128)S(1)} %bitcast.9), kind=kLoop, calls=%fused_computation.101 | loop fusion | flops 2097152 | bytes 9437184 | tf_op jit(solution)/shard_map/div | solution.py:66
  (71 shorter events, 37.8 us)
Async XLA Ops:
  7.2 250.6 %all-gather.3.cloned.1.call-start = ((), (), s32[]{:S(2)}) async-start(), calls=%async_computation | async-start | bytes 3145728 | tf_op jit(solution)/shard_map/all_gather | solution.py:24
  7.2 29.3 %copy-start.1 = (f32[4,64,32,128]{3,2,1,0:T(8,128)S(1)}, f32[4,64,32,128]{3,2,1,0:T(8,128)}, u32[]{:S(2)}) copy-start(f32[4,64,32,128]{3,2,1,0:T(8,128)} %param.4) | copy-start | bytes 12582916
  9.1 27.3 %collective-permute-start = (f32[1,64,32,128]{3,2,1,0:T(8,128)S(1)}, f32[1,64,32,128]{3,2,1,0:T(8,128)S(1)}, u32[]{:S(2)}, u32[]{:S(2)}) collective-permute-start(f32[1,64,32,128]{3,2,1,0:T(8,128)S(1)} %get-tuple-element.142), channel_id=1, source_target_pairs={{0,4},{1,5},{2,6},{3,7},{8,12},{9,13},{10,14},{11,15},{16,20},{17,... | collective-permute-start | bytes 3145736 | tf_op jit(solution)/shard_map/ppermute | solution.py:16
  14.1 26.5 %collective-permute-start.1 = (f32[1,64,32,128]{3,2,1,0:T(8,128)S(1)}, f32[1,64,32,128]{3,2,1,0:T(8,128)S(1)}, u32[]{:S(2)}, u32[]{:S(2)}) collective-permute-start(f32[1,64,32,128]{3,2,1,0:T(8,128)S(1)} %get-tuple-element.141), channel_id=1, source_target_pairs={{4,0},{5,1},{6,2},{7,3},{12,8},{13,9},{14,10},{15,11},{20,16},{21,... | collective-permute-start | bytes 3145736 | tf_op jit(solution)/shard_map/ppermute | solution.py:17
  40.6 17.7 %copy-start.3 = (f32[1,64,32,128]{3,2,1,0:T(8,128)}, f32[1,64,32,128]{3,2,1,0:T(8,128)S(1)}, u32[]{:S(2)}) copy-start(f32[1,64,32,128]{3,2,1,0:T(8,128)S(1)} %collective-permute-done.1) | copy-start | bytes 3145732
  40.7 2.9 %collective-permute-start.2 = (f32[6,1,32,128]{3,2,1,0:T(8,128)S(1)}, f32[6,1,32,128]{3,2,1,0:T(8,128)S(1)}, u32[]{:S(2)}, u32[]{:S(2)}) collective-permute-start(f32[6,1,32,128]{3,2,1,0:T(8,128)S(1)} %get-tuple-element.133), channel_id=1, source_target_pairs={{0,2},{1,3},{4,6},{5,7},{8,10},{9,11},{12,14},{13,15},{16,18},{17,... | collective-permute-start | bytes 294920 | tf_op jit(solution)/shard_map/ppermute | solution.py:16
  42.0 16.5 %copy-start = (f32[4,64,32,128]{3,2,1,0:T(8,128)S(1)}, f32[4,64,32,128]{3,2,1,0:T(8,128)}, u32[]{:S(2)}) copy-start(f32[4,64,32,128]{3,2,1,0:T(8,128)} %param.5) | copy-start | bytes 12582916
  42.0 3.5 %collective-permute-start.3 = (f32[6,1,32,128]{3,2,1,0:T(8,128)S(1)}, f32[6,1,32,128]{3,2,1,0:T(8,128)S(1)}, u32[]{:S(2)}, u32[]{:S(2)}) collective-permute-start(f32[6,1,32,128]{3,2,1,0:T(8,128)S(1)} %get-tuple-element.134), channel_id=1, source_target_pairs={{2,0},{3,1},{6,4},{7,5},{10,8},{11,9},{14,12},{15,13},{18,16},{19,... | collective-permute-start | bytes 294920 | tf_op jit(solution)/shard_map/ppermute | solution.py:17
  45.5 5.1 %copy-start.4 = (f32[6,1,32,128]{3,2,1,0:T(8,128)}, f32[6,1,32,128]{3,2,1,0:T(8,128)S(1)}, u32[]{:S(2)}) copy-start(f32[6,1,32,128]{3,2,1,0:T(8,128)S(1)} %collective-permute-done.3) | copy-start | bytes 294916
  45.8 8.4 %collective-permute-start.4 = (f32[6,66,1,128]{3,1,2,0:T(8,128)S(1)}, f32[6,66,1,128]{3,1,2,0:T(8,128)S(1)}, u32[]{:S(2)}, u32[]{:S(2)}) collective-permute-start(f32[6,66,1,128]{3,1,2,0:T(8,128)S(1)} %copy.23), channel_id=1, source_target_pairs={{0,1},{2,3},{4,5},{6,7},{8,9},{10,11},{12,13},{14,15},{16,17},{18,... | collective-permute-start | bytes 608264 | tf_op jit(solution)/shard_map/ppermute | solution.py:16
  49.2 9.1 %collective-permute-start.5 = (f32[6,66,1,128]{3,1,2,0:T(8,128)S(1)}, f32[6,66,1,128]{3,1,2,0:T(8,128)S(1)}, u32[]{:S(2)}, u32[]{:S(2)}) collective-permute-start(f32[6,66,1,128]{3,1,2,0:T(8,128)S(1)} %copy.25), channel_id=1, source_target_pairs={{1,0},{3,2},{5,4},{7,6},{9,8},{11,10},{13,12},{15,14},{17,16},{19,... | collective-permute-start | bytes 608264 | tf_op jit(solution)/shard_map/ppermute | solution.py:17
  68.0 23.2 %collective-permute-start.6 = (f32[1,64,32,128]{3,2,1,0:T(8,128)S(1)}, f32[1,64,32,128]{3,2,1,0:T(8,128)S(1)}, u32[]{:S(2)}, u32[]{:S(2)}) collective-permute-start(f32[1,64,32,128]{3,2,1,0:T(8,128)S(1)} %get-tuple-element.139), channel_id=1, source_target_pairs={{0,4},{1,5},{2,6},{3,7},{8,12},{9,13},{10,14},{11,15},{16,20},{17,... | collective-permute-start | bytes 3145736 | tf_op jit(solution)/shard_map/ppermute | solution.py:16
  69.5 25.8 %collective-permute-start.7 = (f32[1,64,32,128]{3,2,1,0:T(8,128)S(1)}, f32[1,64,32,128]{3,2,1,0:T(8,128)S(1)}, u32[]{:S(2)}, u32[]{:S(2)}) collective-permute-start(f32[1,64,32,128]{3,2,1,0:T(8,128)S(1)} %get-tuple-element.140), channel_id=1, source_target_pairs={{4,0},{5,1},{6,2},{7,3},{12,8},{13,9},{14,10},{15,11},{20,16},{21,... | collective-permute-start | bytes 3145736 | tf_op jit(solution)/shard_map/ppermute | solution.py:17
  95.3 2.6 collective-permute-start.8
  96.6 3.2 %collective-permute-start.9 = (f32[6,1,32,128]{3,2,1,0:T(8,128)S(1)}, f32[6,1,32,128]{3,2,1,0:T(8,128)S(1)}, u32[]{:S(2)}, u32[]{:S(2)}) collective-permute-start(f32[6,1,32,128]{3,2,1,0:T(8,128)S(1)} %get-tuple-element.132), channel_id=1, source_target_pairs={{2,0},{3,1},{6,4},{7,5},{10,8},{11,9},{14,12},{15,13},{18,16},{19,... | collective-permute-start | bytes 294920 | tf_op jit(solution)/shard_map/ppermute | solution.py:17
  100.1 6.6 %collective-permute-start.10 = (f32[6,66,1,128]{3,1,2,0:T(8,128)S(1)}, f32[6,66,1,128]{3,1,2,0:T(8,128)S(1)}, u32[]{:S(2)}, u32[]{:S(2)}) collective-permute-start(f32[6,66,1,128]{3,1,2,0:T(8,128)S(1)} %copy.27), channel_id=1, source_target_pairs={{0,1},{2,3},{4,5},{6,7},{8,9},{10,11},{12,13},{14,15},{16,17},{18,... | collective-permute-start | bytes 608264 | tf_op jit(solution)/shard_map/ppermute | solution.py:16
  101.6 9.2 %collective-permute-start.11 = (f32[6,66,1,128]{3,1,2,0:T(8,128)S(1)}, f32[6,66,1,128]{3,1,2,0:T(8,128)S(1)}, u32[]{:S(2)}, u32[]{:S(2)}) collective-permute-start(f32[6,66,1,128]{3,1,2,0:T(8,128)S(1)} %copy.29), channel_id=1, source_target_pairs={{1,0},{3,2},{5,4},{7,6},{9,8},{11,10},{13,12},{15,14},{17,16},{19,... | collective-permute-start | bytes 608264 | tf_op jit(solution)/shard_map/ppermute | solution.py:17
  118.5 23.3 %collective-permute-start.12 = (f32[1,64,32,128]{3,2,1,0:T(8,128)S(1)}, f32[1,64,32,128]{3,2,1,0:T(8,128)S(1)}, u32[]{:S(2)}, u32[]{:S(2)}) collective-permute-start(f32[1,64,32,128]{3,2,1,0:T(8,128)S(1)} %get-tuple-element.137), channel_id=1, source_target_pairs={{0,4},{1,5},{2,6},{3,7},{8,12},{9,13},{10,14},{11,15},{16,20},{17,... | collective-permute-start | bytes 3145736 | tf_op jit(solution)/shard_map/ppermute | solution.py:16
  120.0 25.9 %collective-permute-start.13 = (f32[1,64,32,128]{3,2,1,0:T(8,128)S(1)}, f32[1,64,32,128]{3,2,1,0:T(8,128)S(1)}, u32[]{:S(2)}, u32[]{:S(2)}) collective-permute-start(f32[1,64,32,128]{3,2,1,0:T(8,128)S(1)} %get-tuple-element.138), channel_id=1, source_target_pairs={{4,0},{5,1},{6,2},{7,3},{12,8},{13,9},{14,10},{15,11},{20,16},{21,... | collective-permute-start | bytes 3145736 | tf_op jit(solution)/shard_map/ppermute | solution.py:17
  146.0 2.6 collective-permute-start.14
  147.3 3.2 %collective-permute-start.15 = (f32[6,1,32,128]{3,2,1,0:T(8,128)S(1)}, f32[6,1,32,128]{3,2,1,0:T(8,128)S(1)}, u32[]{:S(2)}, u32[]{:S(2)}) collective-permute-start(f32[6,1,32,128]{3,2,1,0:T(8,128)S(1)} %get-tuple-element.130), channel_id=1, source_target_pairs={{2,0},{3,1},{6,4},{7,5},{10,8},{11,9},{14,12},{15,13},{18,16},{19,... | collective-permute-start | bytes 294920 | tf_op jit(solution)/shard_map/ppermute | solution.py:17
  150.8 6.6 %collective-permute-start.16 = (f32[6,66,1,128]{3,1,2,0:T(8,128)S(1)}, f32[6,66,1,128]{3,1,2,0:T(8,128)S(1)}, u32[]{:S(2)}, u32[]{:S(2)}) collective-permute-start(f32[6,66,1,128]{3,1,2,0:T(8,128)S(1)} %copy.31), channel_id=1, source_target_pairs={{0,1},{2,3},{4,5},{6,7},{8,9},{10,11},{12,13},{14,15},{16,17},{18,... | collective-permute-start | bytes 608264 | tf_op jit(solution)/shard_map/ppermute | solution.py:16
  152.3 9.2 %collective-permute-start.17 = (f32[6,66,1,128]{3,1,2,0:T(8,128)S(1)}, f32[6,66,1,128]{3,1,2,0:T(8,128)S(1)}, u32[]{:S(2)}, u32[]{:S(2)}) collective-permute-start(f32[6,66,1,128]{3,1,2,0:T(8,128)S(1)} %copy.33), channel_id=1, source_target_pairs={{1,0},{3,2},{5,4},{7,6},{9,8},{11,10},{13,12},{15,14},{17,16},{19,... | collective-permute-start | bytes 608264 | tf_op jit(solution)/shard_map/ppermute | solution.py:17
  169.1 23.3 %collective-permute-start.18 = (f32[1,64,32,128]{3,2,1,0:T(8,128)S(1)}, f32[1,64,32,128]{3,2,1,0:T(8,128)S(1)}, u32[]{:S(2)}, u32[]{:S(2)}) collective-permute-start(f32[1,64,32,128]{3,2,1,0:T(8,128)S(1)} %get-tuple-element.135), channel_id=1, source_target_pairs={{0,4},{1,5},{2,6},{3,7},{8,12},{9,13},{10,14},{11,15},{16,20},{17,... | collective-permute-start | bytes 3145736 | tf_op jit(solution)/shard_map/ppermute | solution.py:16
  170.6 25.9 %collective-permute-start.19 = (f32[1,64,32,128]{3,2,1,0:T(8,128)S(1)}, f32[1,64,32,128]{3,2,1,0:T(8,128)S(1)}, u32[]{:S(2)}, u32[]{:S(2)}) collective-permute-start(f32[1,64,32,128]{3,2,1,0:T(8,128)S(1)} %get-tuple-element.136), channel_id=1, source_target_pairs={{4,0},{5,1},{6,2},{7,3},{12,8},{13,9},{14,10},{15,11},{20,16},{21,... | collective-permute-start | bytes 3145736 | tf_op jit(solution)/shard_map/ppermute | solution.py:17
  196.6 2.6 collective-permute-start.20
  197.9 3.2 %collective-permute-start.21 = (f32[6,1,32,128]{3,2,1,0:T(8,128)S(1)}, f32[6,1,32,128]{3,2,1,0:T(8,128)S(1)}, u32[]{:S(2)}, u32[]{:S(2)}) collective-permute-start(f32[6,1,32,128]{3,2,1,0:T(8,128)S(1)} %get-tuple-element.128), channel_id=1, source_target_pairs={{2,0},{3,1},{6,4},{7,5},{10,8},{11,9},{14,12},{15,13},{18,16},{19,... | collective-permute-start | bytes 294920 | tf_op jit(solution)/shard_map/ppermute | solution.py:17
  201.4 6.6 %collective-permute-start.22 = (f32[6,66,1,128]{3,1,2,0:T(8,128)S(1)}, f32[6,66,1,128]{3,1,2,0:T(8,128)S(1)}, u32[]{:S(2)}, u32[]{:S(2)}) collective-permute-start(f32[6,66,1,128]{3,1,2,0:T(8,128)S(1)} %copy.35), channel_id=1, source_target_pairs={{0,1},{2,3},{4,5},{6,7},{8,9},{10,11},{12,13},{14,15},{16,17},{18,... | collective-permute-start | bytes 608264 | tf_op jit(solution)/shard_map/ppermute | solution.py:16
  202.9 9.2 %collective-permute-start.23 = (f32[6,66,1,128]{3,1,2,0:T(8,128)S(1)}, f32[6,66,1,128]{3,1,2,0:T(8,128)S(1)}, u32[]{:S(2)}, u32[]{:S(2)}) collective-permute-start(f32[6,66,1,128]{3,1,2,0:T(8,128)S(1)} %copy.37), channel_id=1, source_target_pairs={{1,0},{3,2},{5,4},{7,6},{9,8},{11,10},{13,12},{15,14},{17,16},{19,... | collective-permute-start | bytes 608264 | tf_op jit(solution)/shard_map/ppermute | solution.py:17
  219.5 3.3 %copy-start.2 = (f32[4,64,32,128]{3,2,1,0:T(8,128)}, f32[4,64,32,128]{3,2,1,0:T(8,128)S(1)}, u32[]{:S(2)}) copy-start(f32[4,64,32,128]{3,2,1,0:T(8,128)S(1)} %fusion.4) | copy-start | bytes 12582916
Sparse Core Ops, SparseCore 0:
  225.2 32.4 all-gather.2
where the time goes:
time: 273 us
  waiting for transfers between devices  169 us (62%)
  other arithmetic  43 us (16%)
  starting transfers between devices  38.5 us (14%)
  between operations  14.5 us (5%)
  local copies, waits for them, and re-layouts  7.51 us (3%)
    ppermute x12, waiting for transfers between devices, with_halo(): before = lax.ppermute(last, axis, up)  97.1 us
    ppermute x12, waiting for transfers between devices, with_halo(): after = lax.ppermute(first, axis, down)  39.5 us
    all_gather x1, waiting for transfers between devices, prefix(): everything = lax.all_gather(array, axis)  32.6 us
    add x4, other arithmetic, march_step(): return middle + 0.1 * spread + 0.2 * middle * (1.0 - middle * crowding)  30.9 us
    ppermute x12, starting transfers between devices, with_halo(): before = lax.ppermute(last, axis, up)  22.5 us
    ppermute x12, starting transfers between devices, with_halo(): after = lax.ppermute(first, axis, down)  15.9 us
  transfers between devices with their start and end apart: 25, of which 21 were waited for; matrix products, arithmetic and copies ran while one was open for 1% of the time, Pallas kernels for 0%

commit v1 on v0

v1 whole, which is shorter than its diff:
```python
import functools

import jax
import jax.numpy as jnp
from jax import lax
from jax.experimental import pallas as pl
from jax.experimental.pallas import tpu as pltpu
from jax.sharding import PartitionSpec as P

STEPS = 4
CHUNK = 8
MESH = pl.DeviceIdType.MESH


def kernel(
    sizes,
    tracer_ref,
    crowding_ref,
    column_ref,
    end_ref,
    x,
    crowd,
    sums,
    total,
    below,
    lev_first,
    lev_last,
    lev_lower,
    lev_upper,
    load_sem,
    lat_send,
    lat_recv,
    lon_send,
    lon_recv,
    lev_send,
    lev_recv,
    sum_send,
    sum_recv,
    end_sem,
    column_sem,
):
    J, I, K, L = tracer_ref.shape
    chunks = I // CHUNK
    places = {axis: lax.axis_index(axis) for axis in sizes}
    lower = {axis: places[axis] > 0 for axis in sizes}
    upper = {axis: places[axis] < sizes[axis] - 1 for axis in sizes}

    order = [J - 1, 0] + list(range(1, J - 1))
    loads = []
    for j in order:
        loads.append(pltpu.make_async_copy(tracer_ref.at[j], x.at[0, j + 1, pl.ds(1, I)], load_sem.at[0, j]))
    for j in range(J):
        loads.append(pltpu.make_async_copy(crowding_ref.at[j], crowd.at[j], load_sem.at[1, j]))
    for load in loads:
        load.start()

    barrier = pltpu.get_barrier_semaphore()
    for axis in sizes:
        for there, step in ((lower[axis], -1), (upper[axis], 1)):

            @pl.when(there)
            def _():
                pl.semaphore_signal(barrier, inc=1, device_id={axis: places[axis] + step}, device_id_type=MESH)

    beside = sum(there[axis].astype(jnp.int32) for axis in sizes for there in (lower, upper))
    pl.semaphore_wait(barrier, beside)

    def cells(c):
        return pl.ds(1 + c * CHUNK, CHUNK)

    def lat_copy(r, c, up):
        src, dst = (J, 0) if up else (1, J + 1)
        return pltpu.make_async_remote_copy(
            src_ref=x.at[r, src, cells(c)],
            dst_ref=x.at[r, dst, cells(c)],
            send_sem=lat_send.at[int(up), r, c],
            recv_sem=lat_recv.at[int(up), r, c],
            device_id={"lat": places["lat"] + (1 if up else -1)},
            device_id_type=MESH,
        )

    def lon_copy(r, up):
        src, dst = (I, 0) if up else (1, I + 1)
        return pltpu.make_async_remote_copy(
            src_ref=x.at[r, pl.ds(1, J), src],
            dst_ref=x.at[r, pl.ds(1, J), dst],
            send_sem=lon_send.at[int(up), r],
            recv_sem=lon_recv.at[int(up), r],
            device_id={"lon": places["lon"] + (1 if up else -1)},
            device_id_type=MESH,
        )

    def lev_copy(r, c, up):
        src, dst = (lev_last, lev_lower) if up else (lev_first, lev_upper)
        part = pl.ds(pl.multiple_of(c * CHUNK, CHUNK), CHUNK)
        return pltpu.make_async_remote_copy(
            src_ref=src.at[r, :, part],
            dst_ref=dst.at[r, :, part],
            send_sem=lev_send.at[int(up), r, c],
            recv_sem=lev_recv.at[int(up), r, c],
            device_id={"lev": places["lev"] + (1 if up else -1)},
            device_id_type=MESH,
        )

    def sum_copy(c):
        part = pl.ds(c * CHUNK, CHUNK)
        return pltpu.make_async_remote_copy(
            src_ref=total.at[part],
            dst_ref=below.at[part],
            send_sem=sum_send.at[c],
            recv_sem=sum_recv.at[c],
            device_id={"lat": places["lat"] + 1},
            device_id_type=MESH,
        )

    def end_copy(c):
        return pltpu.make_async_copy(
            x.at[STEPS, pl.ds(1, J), cells(c)], end_ref.at[:, pl.ds(c * CHUNK, CHUNK)], end_sem.at[c]
        )

    def column_copy(c):
        part = pl.ds(c * CHUNK, CHUNK)
        return pltpu.make_async_copy(sums.at[:, part], column_ref.at[:, part], column_sem.at[c])

    def when_do(there, act):
        @pl.when(there)
        def _():
            act()

    def send_lat(r, c):
        when_do(upper["lat"], lambda: lat_copy(r, c, True).start())
        when_do(lower["lat"], lambda: lat_copy(r, c, False).start())

    def send_lev(r, c):
        when_do(upper["lev"], lambda: lev_copy(r, c, True).start())
        when_do(lower["lev"], lambda: lev_copy(r, c, False).start())

    def over(count, body):
        lax.fori_loop(0, count, lambda n, carry: (body(n), carry)[1], 0)

    loads[0].wait()
    when_do(upper["lat"], lambda: over(chunks, lambda c: lat_copy(0, c, True).start()))
    loads[1].wait()
    when_do(lower["lat"], lambda: over(chunks, lambda c: lat_copy(0, c, False).start()))
    for load in loads[2:J]:
        load.wait()
    when_do(upper["lon"], lambda: lon_copy(0, True).start())
    when_do(lower["lon"], lambda: lon_copy(0, False).start())

    def take_edges(c):
        def turn(n):
            i = c * CHUNK + n
            for j in range(J):
                value = x[0, j + 1, i + 1]
                lev_first[0, j, pl.ds(i, 1), :] = value[0:1, :]
                lev_last[0, j, pl.ds(i, 1), :] = value[K - 1 : K, :]

        over(CHUNK, turn)
        send_lev(0, c)

    over(chunks, take_edges)

    def zero_row(row):
        def turn(i):
            x[0, row, i + 1] = jnp.zeros((K, L), jnp.float32)

        over(I, turn)

    def zero_column(column):
        for r in range(STEPS):
            for j in range(J):
                x[r, j + 1, column] = jnp.zeros((K, L), jnp.float32)

    def zero_level(ref):
        for j in range(J):
            ref[0, j] = jnp.zeros((I, L), jnp.float32)

    def zero_below():
        def turn(i):
            below[i] = jnp.zeros((K, L), jnp.float32)

        over(I, turn)

    when_do(jnp.logical_not(lower["lat"]), lambda: zero_row(0))
    when_do(jnp.logical_not(upper["lat"]), lambda: zero_row(J + 1))
    when_do(jnp.logical_not(lower["lon"]), lambda: zero_column(0))
    when_do(jnp.logical_not(upper["lon"]), lambda: zero_column(I + 1))
    when_do(jnp.logical_not(lower["lev"]), lambda: zero_level(lev_lower))
    when_do(jnp.logical_not(upper["lev"]), lambda: zero_level(lev_upper))
    when_do(jnp.logical_not(lower["lat"]), zero_below)
    for load in loads[J:]:
        load.wait()

    level = lax.broadcasted_iota(jnp.int32, (K, L), 0)
    at_first, at_last = level == 0, level == K - 1

    def advance(r, i):
        lat_low = jnp.where(lower["lat"], r, 0)
        lat_high = jnp.where(upper["lat"], r, 0)
        lev_low = jnp.where(lower["lev"], r, 0)
        lev_high = jnp.where(upper["lev"], r, 0)
        rows = [x[lat_low, 0, i + 1]]
        rows += [x[r, j + 1, i + 1] for j in range(J)]
        rows += [x[lat_high, J + 1, i + 1]]
        new = []
        for j in range(J):
            middle = rows[j + 1]
            first = jnp.broadcast_to(lev_lower[lev_low, j, pl.ds(i, 1), :], (K, L))
            last = jnp.broadcast_to(lev_upper[lev_high, j, pl.ds(i, 1), :], (K, L))
            spread = rows[j] + rows[j + 2]
            spread = spread + x[r, j + 1, i] + x[r, j + 1, i + 2]
            spread = spread + jnp.where(at_first, first, pltpu.roll(middle, 1, 0))
            spread = spread + jnp.where(at_last, last, pltpu.roll(middle, K - 1, 0))
            spread = spread - 6.0 * middle
            new.append(middle + 0.1 * spread + 0.2 * middle * (1.0 - middle * crowd[j, i]))
        for j in range(J):
            x[r + 1, j + 1, i + 1] = new[j]
        return new

    def arrive(r, c):
        when_do(lower["lat"], lambda: lat_copy(r, c, True).wait_recv())
        when_do(upper["lat"], lambda: lat_copy(r, c, False).wait_recv())
        when_do(lower["lev"], lambda: lev_copy(r, c, True).wait_recv())
        when_do(upper["lev"], lambda: lev_copy(r, c, False).wait_recv())
        when_do(jnp.logical_and(lower["lon"], c == 0), lambda: lon_copy(r, True).wait_recv())
        when_do(jnp.logical_and(upper["lon"], c == chunks - 1), lambda: lon_copy(r, False).wait_recv())

    def march(n):
        r, c = n // chunks, n % chunks
        arrive(r, c)

        def turn(m):
            i = c * CHUNK + m
            new = advance(r, i)
            for j in range(J):
                lev_first[r + 1, j, pl.ds(i, 1), :] = new[j][0:1, :]
                lev_last[r + 1, j, pl.ds(i, 1), :] = new[j][K - 1 : K, :]

        over(CHUNK, turn)
        send_lat(r + 1, c)
        send_lev(r + 1, c)
        when_do(jnp.logical_and(lower["lon"], c == 0), lambda: lon_copy(r + 1, False).start())
        when_do(jnp.logical_and(upper["lon"], c == chunks - 1), lambda: lon_copy(r + 1, True).start())

    over((STEPS - 1) * chunks, march)

    def finish(c):
        r = STEPS - 1
        arrive(r, c)

        def turn(m):
            i = c * CHUNK + m
            here = None
            for j, value in enumerate(advance(r, i)):
                here = value if here is None else here + value
                sums[j, i] = here
            total[i] = here

        over(CHUNK, turn)
        end_copy(c).start()
        when_do(jnp.logical_not(lower["lat"]), lambda: sum_copy(c).start())

    over(chunks, finish)

    scale = 1.0 / (J * sizes["lat"])

    def conclude(c):
        def pass_on():
            def turn(m):
                i = c * CHUNK + m
                total[i] = total[i] + below[i]

            over(CHUNK, turn)
            sum_copy(c).start()

        when_do(lower["lat"], lambda: sum_copy(c).wait_recv())
        when_do(jnp.logical_and(lower["lat"], upper["lat"]), pass_on)

        def turn(m):
            i = c * CHUNK + m
            before = below[i]
            for j in range(J):
                sums[j, i] = (sums[j, i] + before) * scale

        over(CHUNK, turn)
        column_copy(c).start()

    over(chunks, conclude)

    def sent(n):
        r, c = n // chunks, n % chunks
        when_do(upper["lat"], lambda: lat_copy(r, c, True).wait_send())
        when_do(lower["lat"], lambda: lat_copy(r, c, False).wait_send())
        when_do(upper["lev"], lambda: lev_copy(r, c, True).wait_send())
        when_do(lower["lev"], lambda: lev_copy(r, c, False).wait_send())

    over(STEPS * chunks, sent)

    def sent_lon(r):
        when_do(upper["lon"], lambda: lon_copy(r, True).wait_send())
        when_do(lower["lon"], lambda: lon_copy(r, False).wait_send())

    over(STEPS, sent_lon)

    def ended(c):
        when_do(upper["lat"], lambda: sum_copy(c).wait_send())
        end_copy(c).wait()
        column_copy(c).wait()

    over(chunks, ended)


def on_device(tracer, crowding):
    J, I, K, L = tracer.shape
    sizes = {axis: lax.axis_size(axis) for axis in ("lat", "lon", "lev")}
    chunks = I // CHUNK
    f32, dma = jnp.float32, pltpu.SemaphoreType.DMA
    anywhere = pl.BlockSpec(memory_space=pl.ANY)
    return pl.pallas_call(
        functools.partial(kernel, sizes),
        out_shape=(jax.ShapeDtypeStruct(tracer.shape, f32),) * 2,
        in_specs=[anywhere] * 2,
        out_specs=(anywhere,) * 2,
        scratch_shapes=[
            pltpu.VMEM((STEPS + 1, J + 2, I + 2, K, L), f32),
            pltpu.VMEM((J, I, K, L), f32),
            pltpu.VMEM((J, I, K, L), f32),
            pltpu.VMEM((I, K, L), f32),
            pltpu.VMEM((I, K, L), f32),
            pltpu.VMEM((STEPS, J, I, L), f32),
            pltpu.VMEM((STEPS, J, I, L), f32),
            pltpu.VMEM((STEPS, J, I, L), f32),
            pltpu.VMEM((STEPS, J, I, L), f32),
            dma((2, J)),
            dma((2, STEPS, chunks)),
            dma((2, STEPS, chunks)),
            dma((2, STEPS)),
            dma((2, STEPS)),
            dma((2, STEPS, chunks)),
            dma((2, STEPS, chunks)),
            dma((chunks,)),
            dma((chunks,)),
            dma((chunks,)),
            dma((chunks,)),
        ],
        compiler_params=pltpu.CompilerParams(
            collective_id=0, has_side_effects=True, vmem_limit_bytes=60 * 2**20
        ),
        name="march",
    )(tracer, crowding)


def solution(mesh):
    spec = P(("unit", "lat"), "lon", "lev", None)
    return jax.shard_map(on_device, mesh=mesh, in_specs=(spec, spec), out_specs=(spec, spec), check_vma=False)
```

time: 273 us -> 126 us (0.46)
  waiting for transfers between devices: 169 us -> 0 us
  Pallas kernels: 0 us -> 118 us
  other arithmetic: 43 us -> 0 us
  starting transfers between devices: 38.5 us -> 0 us
  between operations: 14.5 us -> 0.65 us
    ppermute x24 -> x0, waiting for transfers between devices: 137 us -> none  [the longest x12 97.1 us: with_halo(): before = lax.ppermute(last, axis, up)]
    pallas_call x0 -> x1, Pallas kernels: none -> 118 us  [on_device(): pl.pallas_call(functools.partial(kernel, sizes), out_shape=(jax.ShapeDtyp...]
    ppermute x24 -> x0, starting transfers between devices: 38.4 us -> none  [the longest x12 22.5 us: with_halo(): before = lax.ppermute(last, axis, up)]
    all_gather x1 -> x0, waiting for transfers between devices: 32.6 us -> none  [prefix(): everything = lax.all_gather(array, axis)]
    add x4 -> x0, other arithmetic: 30.9 us -> none  [march_step(): return middle + 0.1 * spread + 0.2 * middle * (1.0 - middle * crowding)]
    unnamed x12 -> x4, local copies, waits for them, and re-layouts: 0.95 us -> 6.84 us
    div x1 -> x0, other arithmetic: 4.86 us -> none  [on_device(): column_sum = (here + below) / (tracer.shape[0] * lax.axis_size('lat'))]
    slice x14 -> x0, local copies, waits for them, and re-layouts: 4.82 us -> none  [the longest x1 2.29 us: on_device(): total = lax.slice_in_dim(here, here.shape[0] - 1, here.shape[0], axis=0)]
  transfers between devices with their start and end apart: 25 -> 0, of which waited for: 21 -> 0; matrix products, arithmetic and copies ran while one was open for 1% -> 0% of each run, Pallas kernels for 0% -> 0%
where the time goes in v1:
time: 126 us
  Pallas kernels  118 us (94%)
  local copies, waits for them, and re-layouts  6.84 us (5%)
    pallas_call x1, Pallas kernels, on_device(): pl.pallas_call(functools.partial(kernel, sizes), out_shape=(jax.ShapeDtyp...  118 us
    unnamed x4, local copies, waits for them, and re-layouts  6.84 us

profile of v1, /device:TPU:0, one launch (start us, length us, event | category | flops | bytes accessed | tf_op | source)
XLA Modules:
  0.0 125.6 jit_solution(3302581598366603754)
XLA Ops:
  0.6 118.2 %march.1 = (f32[4,64,32,128]{3,2,1,0:T(8,128)}, f32[4,64,32,128]{3,2,1,0:T(8,128)}) custom-call(f32[4,64,32,128]{3,2,1,0:T(8,128)} %tracer_ref.1, f32[4,64,32,128]{3,2,1,0:T(8,128)} %crowding_ref.1), custom_call_target="tpu_custom_call" | custom-call | tf_op jit(solution)/shard_map/march/pallas_call | solution.py:319
  118.8 0.0 copy-start
  118.8 4.8 %copy.6 = f32[4,64,32,128]{3,2,1,0:T(8,128)} copy(f32[4,64,32,128]{3,2,1,0:T(8,128)} %get-tuple-element.4) | data formatting | bytes 8388608
  123.6 0.0 copy-done
  123.6 2.0 %copy.7 = f32[4,64,32,128]{3,2,1,0:T(8,128)} copy(f32[4,64,32,128]{3,2,1,0:T(8,128)S(1)} %copy-done) | data formatting | bytes 8388608
Async XLA Ops:
  118.8 4.8 %copy-start = (f32[4,64,32,128]{3,2,1,0:T(8,128)S(1)}, f32[4,64,32,128]{3,2,1,0:T(8,128)}, u32[]{:S(2)}) copy-start(f32[4,64,32,128]{3,2,1,0:T(8,128)} %get-tuple-element.5) | copy-start | bytes 12582916

commit v2 on v1

--- a/solution.py
+++ b/solution.py
@@ -16,11 +16,10 @@
     sizes,
     tracer_ref,
     crowding_ref,
-    column_ref,
-    end_ref,
+    sums,
+    end,
     x,
     crowd,
-    sums,
     total,
     below,
     lev_first,
@@ -36,8 +35,6 @@
     lev_recv,
     sum_send,
     sum_recv,
-    end_sem,
-    column_sem,
 ):
     J, I, K, L = tracer_ref.shape
     chunks = I // CHUNK
@@ -51,7 +48,7 @@
         loads.append(pltpu.make_async_copy(tracer_ref.at[j], x.at[0, j + 1, pl.ds(1, I)], load_sem.at[0, j]))
     for j in range(J):
         loads.append(pltpu.make_async_copy(crowding_ref.at[j], crowd.at[j], load_sem.at[1, j]))
-    for load in loads:
+    for load in loads[:2]:
         load.start()
 
     barrier = pltpu.get_barrier_semaphore()
@@ -113,15 +110,6 @@
             device_id_type=MESH,
         )
 
-    def end_copy(c):
-        return pltpu.make_async_copy(
-            x.at[STEPS, pl.ds(1, J), cells(c)], end_ref.at[:, pl.ds(c * CHUNK, CHUNK)], end_sem.at[c]
-        )
-
-    def column_copy(c):
-        part = pl.ds(c * CHUNK, CHUNK)
-        return pltpu.make_async_copy(sums.at[:, part], column_ref.at[:, part], column_sem.at[c])
-
     def when_do(there, act):
         @pl.when(there)
         def _():
@@ -142,6 +130,8 @@
     when_do(upper["lat"], lambda: over(chunks, lambda c: lat_copy(0, c, True).start()))
     loads[1].wait()
     when_do(lower["lat"], lambda: over(chunks, lambda c: lat_copy(0, c, False).start()))
+    for load in loads[2:]:
+        load.start()
     for load in loads[2:J]:
         load.wait()
     when_do(upper["lon"], lambda: lon_copy(0, True).start())
@@ -213,8 +203,6 @@
             spread = spread + jnp.where(at_last, last, pltpu.roll(middle, K - 1, 0))
             spread = spread - 6.0 * middle
             new.append(middle + 0.1 * spread + 0.2 * middle * (1.0 - middle * crowd[j, i]))
-        for j in range(J):
-            x[r + 1, j + 1, i + 1] = new[j]
         return new
 
     def arrive(r, c):
@@ -233,6 +221,7 @@
             i = c * CHUNK + m
             new = advance(r, i)
             for j in range(J):
+                x[r + 1, j + 1, i + 1] = new[j]
                 lev_first[r + 1, j, pl.ds(i, 1), :] = new[j][0:1, :]
                 lev_last[r + 1, j, pl.ds(i, 1), :] = new[j][K - 1 : K, :]
 
@@ -252,12 +241,12 @@
             i = c * CHUNK + m
             here = None
             for j, value in enumerate(advance(r, i)):
+                end[j, i] = value
                 here = value if here is None else here + value
                 sums[j, i] = here
             total[i] = here
 
         over(CHUNK, turn)
-        end_copy(c).start()
         when_do(jnp.logical_not(lower["lat"]), lambda: sum_copy(c).start())
 
     over(chunks, finish)
@@ -283,7 +272,6 @@
                 sums[j, i] = (sums[j, i] + before) * scale
 
         over(CHUNK, turn)
-        column_copy(c).start()
 
     over(chunks, conclude)
 
@@ -303,11 +291,20 @@
     over(STEPS, sent_lon)
 
     def ended(c):
-        when_do(upper["lat"], lambda: sum_copy(c).wait_send())
-        end_copy(c).wait()
-        column_copy(c).wait()
-
-    over(chunks, ended)
+        sum_copy(c).wait_send()
+
+    when_do(upper["lat"], lambda: over(chunks, ended))
+
+
+def write_out(sums, end, column_ref, end_ref, sem):
+    copies = []
+    for j in range(sums.shape[0]):
+        copies.append(pltpu.make_async_copy(sums.at[j], column_ref.at[j], sem.at[0, j]))
+        copies.append(pltpu.make_async_copy(end.at[j], end_ref.at[j], sem.at[1, j]))
+    for copy in copies:
+        copy.start()
+    for copy in copies:
+        copy.wait()
 
 
 def on_device(tracer, crowding):
@@ -315,15 +312,15 @@
     sizes = {axis: lax.axis_size(axis) for axis in ("lat", "lon", "lev")}
     chunks = I // CHUNK
     f32, dma = jnp.float32, pltpu.SemaphoreType.DMA
-    anywhere = pl.BlockSpec(memory_space=pl.ANY)
-    return pl.pallas_call(
+    anywhere = pl.BlockSpec(memory_space=pltpu.HBM)
+    inside = pl.BlockSpec(memory_space=pltpu.VMEM)
+    results = pl.pallas_call(
         functools.partial(kernel, sizes),
-        out_shape=(jax.ShapeDtypeStruct(tracer.shape, f32),) * 2,
+        out_shape=(pltpu.VMEM(tracer.shape, f32),) * 2,
         in_specs=[anywhere] * 2,
-        out_specs=(anywhere,) * 2,
+        out_specs=(inside,) * 2,
         scratch_shapes=[
-            pltpu.VMEM((STEPS + 1, J + 2, I + 2, K, L), f32),
-            pltpu.VMEM((J, I, K, L), f32),
+            pltpu.VMEM((STEPS, J + 2, I + 2, K, L), f32),
             pltpu.VMEM((J, I, K, L), f32),
             pltpu.VMEM((I, K, L), f32),
             pltpu.VMEM((I, K, L), f32),
@@ -340,14 +337,21 @@
             dma((2, STEPS, chunks)),
             dma((chunks,)),
             dma((chunks,)),
-            dma((chunks,)),
-            dma((chunks,)),
         ],
         compiler_params=pltpu.CompilerParams(
-            collective_id=0, has_side_effects=True, vmem_limit_bytes=60 * 2**20
+            collective_id=0, has_side_effects=True, vmem_limit_bytes=52 * 2**20
         ),
         name="march",
     )(tracer, crowding)
+    return pl.pallas_call(
+        write_out,
+        out_shape=(jax.ShapeDtypeStruct(tracer.shape, f32),) * 2,
+        in_specs=[inside] * 2,
+        out_specs=(anywhere,) * 2,
+        scratch_shapes=[dma((2, J))],
+        compiler_params=pltpu.CompilerParams(vmem_limit_bytes=2**20),
+        name="write_out",
+    )(*results)
 
 
 def solution(mesh):

time: 126 us -> 122 us (0.968)
  local copies, waits for them, and re-layouts: 6.84 us -> 0 us
  Pallas kernels: 118 us -> 121 us
    unnamed x4 -> x0, local copies, waits for them, and re-layouts: 6.84 us -> none
    pallas_call x1 -> x2, Pallas kernels: 118 us -> 121 us  [the longest x1 118 us: on_device(): pl.pallas_call(functools.partial(kernel, sizes), out_shape=(pltpu.VMEM(tr...]
where the time goes in v2:
time: 122 us
  Pallas kernels  121 us (99%)
    pallas_call x1, Pallas kernels, on_device(): pl.pallas_call(functools.partial(kernel, sizes), out_shape=(pltpu.VMEM(tr...  118 us
    pallas_call x1, Pallas kernels, on_device(): pl.pallas_call(write_out, out_shape=(jax.ShapeDtypeStruct(tracer.shape, f...  3.37 us

profile of v2, /device:TPU:0, one launch (start us, length us, event | category | flops | bytes accessed | tf_op | source)
XLA Modules:
  0.0 122.0 jit_solution(1913238482478822359)
XLA Ops:
  0.6 118.0 %march.1 = (f32[4,64,32,128]{3,2,1,0:T(8,128)S(1)}, f32[4,64,32,128]{3,2,1,0:T(8,128)S(1)}) custom-call(f32[4,64,32,128]{3,2,1,0:T(8,128)} %tracer_ref.1, f32[4,64,32,128]{3,2,1,0:T(8,128)} %crowding_ref.1), custom_call_target="tpu_custom_call" | custom-call | tf_op jit(solution)/shard_map/march/pallas_call | solution.py:317
  118.6 3.4 %write_out.1 = (f32[4,64,32,128]{3,2,1,0:T(8,128)}, f32[4,64,32,128]{3,2,1,0:T(8,128)}) custom-call(f32[4,64,32,128]{3,2,1,0:T(8,128)S(1)} %get-tuple-element.4.sums, f32[4,64,32,128]{3,2,1,0:T(8,128)S(1)} %get-tuple-element.5.end), custom_call_target="tpu_custom_call" | custom-call | tf_op jit(solution)/shard_map/write_out/pallas_call | solution.py:346

commit v3 on v2

--- a/solution.py
+++ b/solution.py
@@ -8,7 +8,8 @@
 from jax.sharding import PartitionSpec as P
 
 STEPS = 4
-CHUNK = 8
+PIECES = 2
+OUT_PIECES = 4
 MESH = pl.DeviceIdType.MESH
 
 
@@ -16,12 +17,11 @@
     sizes,
     tracer_ref,
     crowding_ref,
-    sums,
     end,
+    below,
     x,
     crowd,
     total,
-    below,
     lev_first,
     lev_last,
     lev_lower,
@@ -37,7 +37,8 @@
     sum_recv,
 ):
     J, I, K, L = tracer_ref.shape
-    chunks = I // CHUNK
+    chunks = PIECES
+    CHUNK = I // PIECES
     places = {axis: lax.axis_index(axis) for axis in sizes}
     lower = {axis: places[axis] > 0 for axis in sizes}
     upper = {axis: places[axis] < sizes[axis] - 1 for axis in sizes}
@@ -243,37 +244,12 @@
             for j, value in enumerate(advance(r, i)):
                 end[j, i] = value
                 here = value if here is None else here + value
-                sums[j, i] = here
             total[i] = here
 
         over(CHUNK, turn)
         when_do(jnp.logical_not(lower["lat"]), lambda: sum_copy(c).start())
 
     over(chunks, finish)
-
-    scale = 1.0 / (J * sizes["lat"])
-
-    def conclude(c):
-        def pass_on():
-            def turn(m):
-                i = c * CHUNK + m
-                total[i] = total[i] + below[i]
-
-            over(CHUNK, turn)
-            sum_copy(c).start()
-
-        when_do(lower["lat"], lambda: sum_copy(c).wait_recv())
-        when_do(jnp.logical_and(lower["lat"], upper["lat"]), pass_on)
-
-        def turn(m):
-            i = c * CHUNK + m
-            before = below[i]
-            for j in range(J):
-                sums[j, i] = (sums[j, i] + before) * scale
-
-        over(CHUNK, turn)
-
-    over(chunks, conclude)
 
     def sent(n):
         r, c = n // chunks, n % chunks
@@ -290,39 +266,71 @@
 
     over(STEPS, sent_lon)
 
-    def ended(c):
-        sum_copy(c).wait_send()
-
-    when_do(upper["lat"], lambda: over(chunks, ended))
-
-
-def write_out(sums, end, column_ref, end_ref, sem):
-    copies = []
-    for j in range(sums.shape[0]):
-        copies.append(pltpu.make_async_copy(sums.at[j], column_ref.at[j], sem.at[0, j]))
-        copies.append(pltpu.make_async_copy(end.at[j], end_ref.at[j], sem.at[1, j]))
-    for copy in copies:
-        copy.start()
-    for copy in copies:
-        copy.wait()
+    def take_sum(c):
+        def pass_on():
+            def turn(m):
+                i = c * CHUNK + m
+                total[i] = total[i] + below[i]
+
+            over(CHUNK, turn)
+            sum_copy(c).start()
+
+        sum_copy(c).wait_recv()
+        when_do(upper["lat"], pass_on)
+
+    when_do(lower["lat"], lambda: over(chunks, take_sum))
+    when_do(upper["lat"], lambda: over(chunks, lambda c: sum_copy(c).wait_send()))
+
+
+def write_out(scale, end, below, column_ref, end_ref, sums, sem):
+    J, I, K, L = end.shape
+    length = I // OUT_PIECES
+
+    def end_copy(j):
+        return pltpu.make_async_copy(end.at[j], end_ref.at[j], sem.at[0, j])
+
+    def column_copy(c):
+        part = pl.ds(c * length, length)
+        return pltpu.make_async_copy(sums.at[:, part], column_ref.at[:, part], sem.at[1, c])
+
+    for j in range(J):
+        end_copy(j).start()
+
+    def piece(c, carry):
+        def turn(m, carry):
+            i = c * length + m
+            here = below[i]
+            for j in range(J):
+                here = here + end[j, i]
+                sums[j, i] = here * scale
+            return carry
+
+        lax.fori_loop(0, length, turn, 0)
+        column_copy(c).start()
+        return carry
+
+    lax.fori_loop(0, OUT_PIECES, piece, 0)
+    for j in range(J):
+        end_copy(j).wait()
+    for c in range(OUT_PIECES):
+        column_copy(c).wait()
 
 
 def on_device(tracer, crowding):
     J, I, K, L = tracer.shape
     sizes = {axis: lax.axis_size(axis) for axis in ("lat", "lon", "lev")}
-    chunks = I // CHUNK
+    chunks = PIECES
     f32, dma = jnp.float32, pltpu.SemaphoreType.DMA
     anywhere = pl.BlockSpec(memory_space=pltpu.HBM)
     inside = pl.BlockSpec(memory_space=pltpu.VMEM)
     results = pl.pallas_call(
         functools.partial(kernel, sizes),
-        out_shape=(pltpu.VMEM(tracer.shape, f32),) * 2,
+        out_shape=(pltpu.VMEM(tracer.shape, f32), pltpu.VMEM((I, K, L), f32)),
         in_specs=[anywhere] * 2,
         out_specs=(inside,) * 2,
         scratch_shapes=[
             pltpu.VMEM((STEPS, J + 2, I + 2, K, L), f32),
             pltpu.VMEM((J, I, K, L), f32),
-            pltpu.VMEM((I, K, L), f32),
             pltpu.VMEM((I, K, L), f32),
             pltpu.VMEM((STEPS, J, I, L), f32),
             pltpu.VMEM((STEPS, J, I, L), f32),
@@ -344,12 +352,12 @@
         name="march",
     )(tracer, crowding)
     return pl.pallas_call(
-        write_out,
+        functools.partial(write_out, 1.0 / (J * sizes["lat"])),
         out_shape=(jax.ShapeDtypeStruct(tracer.shape, f32),) * 2,
         in_specs=[inside] * 2,
         out_specs=(anywhere,) * 2,
-        scratch_shapes=[dma((2, J))],
-        compiler_params=pltpu.CompilerParams(vmem_limit_bytes=2**20),
+        scratch_shapes=[pltpu.VMEM(tracer.shape, f32), dma((2, max(J, OUT_PIECES)))],
+        compiler_params=pltpu.CompilerParams(vmem_limit_bytes=8 * 2**20),
         name="write_out",
     )(*results)
 

time: 122 us -> 120 us (0.984)
    pallas_call x1, Pallas kernels: 118 us -> 116 us  [on_device(): pl.pallas_call(functools.partial(kernel, sizes), out_shape=(pltpu.VMEM(tr...]
where the time goes in v3:
time: 120 us
  Pallas kernels  120 us (100%)
    pallas_call x1, Pallas kernels, on_device(): pl.pallas_call(functools.partial(kernel, sizes), out_shape=(pltpu.VMEM(tr...  116 us
    pallas_call x1, Pallas kernels, on_device(): pl.pallas_call(functools.partial(write_out, 1.0 / (J * sizes['lat'])), ou...  3.37 us

profile of v3, /device:TPU:0, one launch (start us, length us, event | category | flops | bytes accessed | tf_op | source)
XLA Modules:
  0.0 120.2 jit_solution(6466461179246692302)
XLA Ops:
  0.6 116.2 %march.1 = (f32[4,64,32,128]{3,2,1,0:T(8,128)S(1)}, f32[64,32,128]{2,1,0:T(8,128)S(1)}) custom-call(f32[4,64,32,128]{3,2,1,0:T(8,128)} %tracer_ref.1, f32[4,64,32,128]{3,2,1,0:T(8,128)} %crowding_ref.1), custom_call_target="tpu_custom_call" | custom-call | tf_op jit(solution)/shard_map/march/pallas_call | solution.py:326
  116.8 3.4 %write_out.1 = (f32[4,64,32,128]{3,2,1,0:T(8,128)}, f32[4,64,32,128]{3,2,1,0:T(8,128)}) custom-call(f32[4,64,32,128]{3,2,1,0:T(8,128)S(1)} %get-tuple-element.4.end, f32[64,32,128]{2,1,0:T(8,128)S(1)} %get-tuple-element.5.below), custom_call_target="tpu_custom_call" | custom-call | tf_op jit(solution)/shard_map/write_out/pallas_call | solution.py:354

commit v4 on v0

v4 whole, which is shorter than its diff:
```python
import functools

import jax
import jax.numpy as jnp
from jax import lax
from jax.experimental import pallas as pl
from jax.experimental.pallas import tpu as pltpu
from jax.sharding import PartitionSpec as P

STEPS = 4
PIECES = 2
OUT_PIECES = 4
MESH = pl.DeviceIdType.MESH


def kernel(
    sizes,
    tracer_ref,
    crowding_ref,
    end,
    below,
    x,
    crowd,
    total,
    lev_first,
    lev_last,
    lev_lower,
    lev_upper,
    load_sem,
    lat_send,
    lat_recv,
    lon_send,
    lon_recv,
    lev_send,
    lev_recv,
    sum_send,
    sum_recv,
):
    J, I, K, L = tracer_ref.shape
    chunks = PIECES
    places = {axis: lax.axis_index(axis) for axis in sizes}
    lower = {axis: places[axis] > 0 for axis in sizes}
    upper = {axis: places[axis] < sizes[axis] - 1 for axis in sizes}

    order = [J - 1, 0] + list(range(1, J - 1))
    loads = []
    for j in order:
        loads.append(pltpu.make_async_copy(tracer_ref.at[j], x.at[0, j + 1, pl.ds(1, I)], load_sem.at[0, j]))
    for j in range(J):
        loads.append(pltpu.make_async_copy(crowding_ref.at[j], crowd.at[j], load_sem.at[1, j]))
    for load in loads[:2]:
        load.start()

    barrier = pltpu.get_barrier_semaphore()
    for axis in sizes:
        for there, step in ((lower[axis], -1), (upper[axis], 1)):

            @pl.when(there)
            def _():
                pl.semaphore_signal(barrier, inc=1, device_id={axis: places[axis] + step}, device_id_type=MESH)

    beside = sum(there[axis].astype(jnp.int32) for axis in sizes for there in (lower, upper))
    pl.semaphore_wait(barrier, beside)

    def rounds(length):
        first = (0, length[0])

        def cells(c):
            return pl.ds(1 + first[c], length[c])

        def lat_copy(r, c, up):
            src, dst = (J, 0) if up else (1, J + 1)
            return pltpu.make_async_remote_copy(
                src_ref=x.at[r, src, cells(c)],
                dst_ref=x.at[r, dst, cells(c)],
                send_sem=lat_send.at[int(up), r, c],
                recv_sem=lat_recv.at[int(up), r, c],
                device_id={"lat": places["lat"] + (1 if up else -1)},
                device_id_type=MESH,
            )

        def lon_copy(r, up):
            src, dst = (I, 0) if up else (1, I + 1)
            return pltpu.make_async_remote_copy(
                src_ref=x.at[r, pl.ds(1, J), src],
                dst_ref=x.at[r, pl.ds(1, J), dst],
                send_sem=lon_send.at[int(up), r],
                recv_sem=lon_recv.at[int(up), r],
                device_id={"lon": places["lon"] + (1 if up else -1)},
                device_id_type=MESH,
            )

        def lev_copy(r, c, up):
            src, dst = (lev_last, lev_lower) if up else (lev_first, lev_upper)
            part = pl.ds(first[c], length[c])
            return pltpu.make_async_remote_copy(
                src_ref=src.at[r, :, part],
                dst_ref=dst.at[r, :, part],
                send_sem=lev_send.at[int(up), r, c],
                recv_sem=lev_recv.at[int(up), r, c],
                device_id={"lev": places["lev"] + (1 if up else -1)},
                device_id_type=MESH,
            )

        def sum_copy(c):
            part = pl.ds(first[c], length[c])
            return pltpu.make_async_remote_copy(
                src_ref=total.at[part],
                dst_ref=below.at[part],
                send_sem=sum_send.at[c],
                recv_sem=sum_recv.at[c],
                device_id={"lat": places["lat"] + 1},
                device_id_type=MESH,
            )

        def when_do(there, act):
            @pl.when(there)
            def _():
                act()

        def send_lat(r, c):
            when_do(upper["lat"], lambda: lat_copy(r, c, True).start())
            when_do(lower["lat"], lambda: lat_copy(r, c, False).start())

        def send_lev(r, c):
            when_do(upper["lev"], lambda: lev_copy(r, c, True).start())
            when_do(lower["lev"], lambda: lev_copy(r, c, False).start())

        def each(body):
            for c in range(chunks):
                body(c)

        def over(count, body):
            lax.fori_loop(0, count, lambda n, carry: (body(n), carry)[1], 0)

        loads[0].wait()
        when_do(upper["lat"], lambda: each(lambda c: lat_copy(0, c, True).start()))
        loads[1].wait()
        when_do(lower["lat"], lambda: each(lambda c: lat_copy(0, c, False).start()))
        for load in loads[2:]:
            load.start()
        for load in loads[2:J]:
            load.wait()
        when_do(upper["lon"], lambda: lon_copy(0, True).start())
        when_do(lower["lon"], lambda: lon_copy(0, False).start())

        def take_edges(c):
            def turn(n):
                i = first[c] + n
                for j in range(J):
                    value = x[0, j + 1, i + 1]
                    lev_first[0, j, pl.ds(i, 1), :] = value[0:1, :]
                    lev_last[0, j, pl.ds(i, 1), :] = value[K - 1 : K, :]

            over(length[c], turn)
            send_lev(0, c)

        each(take_edges)

        def zero_row(row):
            def turn(i):
                x[0, row, i + 1] = jnp.zeros((K, L), jnp.float32)

            over(I, turn)

        def zero_column(column):
            for r in range(STEPS):
                for j in range(J):
                    x[r, j + 1, column] = jnp.zeros((K, L), jnp.float32)

        def zero_level(ref):
            for j in range(J):
                ref[0, j] = jnp.zeros((I, L), jnp.float32)

        def zero_below():
            def turn(i):
                below[i] = jnp.zeros((K, L), jnp.float32)

            over(I, turn)

        when_do(jnp.logical_not(lower["lat"]), lambda: zero_row(0))
        when_do(jnp.logical_not(upper["lat"]), lambda: zero_row(J + 1))
        when_do(jnp.logical_not(lower["lon"]), lambda: zero_column(0))
        when_do(jnp.logical_not(upper["lon"]), lambda: zero_column(I + 1))
        when_do(jnp.logical_not(lower["lev"]), lambda: zero_level(lev_lower))
        when_do(jnp.logical_not(upper["lev"]), lambda: zero_level(lev_upper))
        when_do(jnp.logical_not(lower["lat"]), zero_below)
        for load in loads[J:]:
            load.wait()

        level = lax.broadcasted_iota(jnp.int32, (K, L), 0)
        at_first, at_last = level == 0, level == K - 1

        def advance(r, i):
            lat_low = jnp.where(lower["lat"], r, 0)
            lat_high = jnp.where(upper["lat"], r, 0)
            lev_low = jnp.where(lower["lev"], r, 0)
            lev_high = jnp.where(upper["lev"], r, 0)
            rows = [x[lat_low, 0, i + 1]]
            rows += [x[r, j + 1, i + 1] for j in range(J)]
            rows += [x[lat_high, J + 1, i + 1]]
            new = []
            for j in range(J):
                middle = rows[j + 1]
                first = jnp.broadcast_to(lev_lower[lev_low, j, pl.ds(i, 1), :], (K, L))
                last = jnp.broadcast_to(lev_upper[lev_high, j, pl.ds(i, 1), :], (K, L))
                spread = rows[j] + rows[j + 2]
                spread = spread + x[r, j + 1, i] + x[r, j + 1, i + 2]
                spread = spread + jnp.where(at_first, first, pltpu.roll(middle, 1, 0))
                spread = spread + jnp.where(at_last, last, pltpu.roll(middle, K - 1, 0))
                spread = spread - 6.0 * middle
                new.append(middle + 0.1 * spread + 0.2 * middle * (1.0 - middle * crowd[j, i]))
            return new

        def arrive(r, c):
            when_do(lower["lat"], lambda: lat_copy(r, c, True).wait_recv())
            when_do(upper["lat"], lambda: lat_copy(r, c, False).wait_recv())
            when_do(lower["lev"], lambda: lev_copy(r, c, True).wait_recv())
            when_do(upper["lev"], lambda: lev_copy(r, c, False).wait_recv())
            c == 0 and when_do(lower["lon"], lambda: lon_copy(r, True).wait_recv())
            c == chunks - 1 and when_do(upper["lon"], lambda: lon_copy(r, False).wait_recv())

        def march(r, c):
            arrive(r, c)

            def turn(m):
                i = first[c] + m
                new = advance(r, i)
                for j in range(J):
                    x[r + 1, j + 1, i + 1] = new[j]
                    lev_first[r + 1, j, pl.ds(i, 1), :] = new[j][0:1, :]
                    lev_last[r + 1, j, pl.ds(i, 1), :] = new[j][K - 1 : K, :]

            over(length[c], turn)
            send_lat(r + 1, c)
            send_lev(r + 1, c)
            c == 0 and when_do(lower["lon"], lambda: lon_copy(r + 1, False).start())
            c == chunks - 1 and when_do(upper["lon"], lambda: lon_copy(r + 1, True).start())

        over(STEPS - 1, lambda r: each(lambda c: march(r, c)))

        def finish(c):
            r = STEPS - 1
            arrive(r, c)

            def turn(m):
                i = first[c] + m
                here = None
                for j, value in enumerate(advance(r, i)):
                    end[j, i] = value
                    here = value if here is None else here + value
                total[i] = here

            over(length[c], turn)
            when_do(jnp.logical_not(lower["lat"]), lambda: sum_copy(c).start())

        each(finish)

        def sent(r, c):
            when_do(upper["lat"], lambda: lat_copy(r, c, True).wait_send())
            when_do(lower["lat"], lambda: lat_copy(r, c, False).wait_send())
            when_do(upper["lev"], lambda: lev_copy(r, c, True).wait_send())
            when_do(lower["lev"], lambda: lev_copy(r, c, False).wait_send())

        over(STEPS, lambda r: each(lambda c: sent(r, c)))

        def sent_lon(r):
            when_do(upper["lon"], lambda: lon_copy(r, True).wait_send())
            when_do(lower["lon"], lambda: lon_copy(r, False).wait_send())

        over(STEPS, sent_lon)

        def take_sum(c):
            def pass_on():
                def turn(m):
                    i = first[c] + m
                    total[i] = total[i] + below[i]

                over(length[c], turn)
                sum_copy(c).start()

            sum_copy(c).wait_recv()
            when_do(upper["lat"], pass_on)

        when_do(lower["lat"], lambda: each(take_sum))
        when_do(upper["lat"], lambda: each(lambda c: sum_copy(c).wait_send()))

    short = I // 8 * 3

    @pl.when(places["lon"] % 2 == 0)
    def _():
        rounds((I - short, short))

    @pl.when(places["lon"] % 2 == 1)
    def _():
        rounds((short, I - short))


def write_out(scale, end, below, column_ref, end_ref, sums, sem):
    J, I, K, L = end.shape
    length = I // OUT_PIECES

    def end_copy(j):
        return pltpu.make_async_copy(end.at[j], end_ref.at[j], sem.at[0, j])

    def column_copy(c):
        part = pl.ds(c * length, length)
        return pltpu.make_async_copy(sums.at[:, part], column_ref.at[:, part], sem.at[1, c])

    for j in range(J):
        end_copy(j).start()

    def piece(c, carry):
        def turn(m, carry):
            i = c * length + m
            here = below[i]
            for j in range(J):
                here = here + end[j, i]
                sums[j, i] = here * scale
            return carry

        lax.fori_loop(0, length, turn, 0)
        column_copy(c).start()
        return carry

    lax.fori_loop(0, OUT_PIECES, piece, 0)
    for j in range(J):
        end_copy(j).wait()
    for c in range(OUT_PIECES):
        column_copy(c).wait()


def on_device(tracer, crowding):
    J, I, K, L = tracer.shape
    sizes = {axis: lax.axis_size(axis) for axis in ("lat", "lon", "lev")}
    chunks = PIECES
    f32, dma = jnp.float32, pltpu.SemaphoreType.DMA
    anywhere = pl.BlockSpec(memory_space=pltpu.HBM)
    inside = pl.BlockSpec(memory_space=pltpu.VMEM)
    results = pl.pallas_call(
        functools.partial(kernel, sizes),
        out_shape=(pltpu.VMEM(tracer.shape, f32), pltpu.VMEM((I, K, L), f32)),
        in_specs=[anywhere] * 2,
        out_specs=(inside,) * 2,
        scratch_shapes=[
            pltpu.VMEM((STEPS, J + 2, I + 2, K, L), f32),
            pltpu.VMEM((J, I, K, L), f32),
            pltpu.VMEM((I, K, L), f32),
            pltpu.VMEM((STEPS, J, I, L), f32),
            pltpu.VMEM((STEPS, J, I, L), f32),
            pltpu.VMEM((STEPS, J, I, L), f32),
            pltpu.VMEM((STEPS, J, I, L), f32),
            dma((2, J)),
            dma((2, STEPS, chunks)),
            dma((2, STEPS, chunks)),
            dma((2, STEPS)),
            dma((2, STEPS)),
            dma((2, STEPS, chunks)),
            dma((2, STEPS, chunks)),
            dma((chunks,)),
            dma((chunks,)),
        ],
        compiler_params=pltpu.CompilerParams(
            collective_id=0, has_side_effects=True, vmem_limit_bytes=52 * 2**20
        ),
        name="march",
    )(tracer, crowding)
    return pl.pallas_call(
        functools.partial(write_out, 1.0 / (J * sizes["lat"])),
        out_shape=(jax.ShapeDtypeStruct(tracer.shape, f32),) * 2,
        in_specs=[inside] * 2,
        out_specs=(anywhere,) * 2,
        scratch_shapes=[pltpu.VMEM(tracer.shape, f32), dma((2, max(J, OUT_PIECES)))],
        compiler_params=pltpu.CompilerParams(vmem_limit_bytes=8 * 2**20),
        name="write_out",
    )(*results)


def solution(mesh):
    spec = P(("unit", "lat"), "lon", "lev", None)
    return jax.shard_map(on_device, mesh=mesh, in_specs=(spec, spec), out_specs=(spec, spec), check_vma=False)
```

time: 273 us -> 120 us (0.44)
  waiting for transfers between devices: 169 us -> 0 us
  Pallas kernels: 0 us -> 120 us
  other arithmetic: 43 us -> 0 us
  starting transfers between devices: 38.5 us -> 0 us
  between operations: 14.5 us -> 0.64 us
  local copies, waits for them, and re-layouts: 7.51 us -> 0 us
    ppermute x24 -> x0, waiting for transfers between devices: 137 us -> none  [the longest x12 97.1 us: with_halo(): before = lax.ppermute(last, axis, up)]
    pallas_call x0 -> x2, Pallas kernels: none -> 120 us  [the longest x1 116 us: on_device(): pl.pallas_call(functools.partial(kernel, sizes), out_shape=(pltpu.VMEM(tr...]
    ppermute x24 -> x0, starting transfers between devices: 38.4 us -> none  [the longest x12 22.5 us: with_halo(): before = lax.ppermute(last, axis, up)]
    all_gather x1 -> x0, waiting for transfers between devices: 32.6 us -> none  [prefix(): everything = lax.all_gather(array, axis)]
    add x4 -> x0, other arithmetic: 30.9 us -> none  [march_step(): return middle + 0.1 * spread + 0.2 * middle * (1.0 - middle * crowding)]
    div x1 -> x0, other arithmetic: 4.86 us -> none  [on_device(): column_sum = (here + below) / (tracer.shape[0] * lax.axis_size('lat'))]
    slice x14 -> x0, local copies, waits for them, and re-layouts: 4.82 us -> none  [the longest x1 2.29 us: on_device(): total = lax.slice_in_dim(here, here.shape[0] - 1, here.shape[0], axis=0)]
    select_n x2 -> x0, other arithmetic: 3.18 us -> none  [turn(): return jnp.where(reached, new, before)]
  transfers between devices with their start and end apart: 25 -> 0, of which waited for: 21 -> 0; matrix products, arithmetic and copies ran while one was open for 1% -> 0% of each run, Pallas kernels for 0% -> 0%
where the time goes in v4:
time: 120 us
  Pallas kernels  120 us (100%)
    pallas_call x1, Pallas kernels, on_device(): pl.pallas_call(functools.partial(kernel, sizes), out_shape=(pltpu.VMEM(tr...  116 us
    pallas_call x1, Pallas kernels, on_device(): pl.pallas_call(functools.partial(write_out, 1.0 / (J * sizes['lat'])), ou...  3.37 us

profile of v4, /device:TPU:0, one launch (start us, length us, event | category | flops | bytes accessed | tf_op | source)
XLA Modules:
  0.0 120.2 jit_solution(9787582022437995251)
XLA Ops:
  0.6 116.2 %march.1 = (f32[4,64,32,128]{3,2,1,0:T(8,128)S(1)}, f32[64,32,128]{2,1,0:T(8,128)S(1)}) custom-call(f32[4,64,32,128]{3,2,1,0:T(8,128)} %tracer_ref.1, f32[4,64,32,128]{3,2,1,0:T(8,128)} %crowding_ref.1), custom_call_target="tpu_custom_call" | custom-call | tf_op jit(solution)/shard_map/march/pallas_call | solution.py:340
  116.8 3.4 %write_out.1 = (f32[4,64,32,128]{3,2,1,0:T(8,128)}, f32[4,64,32,128]{3,2,1,0:T(8,128)}) custom-call(f32[4,64,32,128]{3,2,1,0:T(8,128)S(1)} %get-tuple-element.4.end, f32[64,32,128]{2,1,0:T(8,128)S(1)} %get-tuple-element.5.below), custom_call_target="tpu_custom_call" | custom-call | tf_op jit(solution)/shard_map/write_out/pallas_call | solution.py:368
